TPU v7x, 128 devices: a whole 4x4x4 slice. The times are simulated.
128 devices in a mesh: blk: 32 (over z, x, core), rows: 4 (over y).
Axes of the slice: x: 4, y: 4, z: 4, core: 2. Of those that a mesh axis runs over, the one named last changes fastest.
Arguments:
- columns: float32 [2048, 16384], P('blk', 'rows'), may hold values from -100 to 100
- plan: int32 [3, 64], replicated, may hold values from 0 to 63, as said below
Outputs:
- swept: float32 [2048, 16384], P('blk', 'rows')
- off_ratio: float32 [3], replicated
Inputs may be any that keep to these rules, and one draw needn't show every extreme that they name: `plan`: row s is a permutation of the 64 positions (position k is slot k % 2 of blk index k // 2). In each row there are a slot t and a number m of 1 to 31 such that the block in slot t of every blk index i goes to slot t of blk index (i + m) modulo 64 / 2, and every other block stays where it is.
All inputs are finite; a program needn't handle non-finite values. Where the computation divides by a largest or mean magnitude, that divisor is 1e-20 or more.
Results may differ from a plain program's by a relative error of at most 0.00011.
Values sent between devices are 32-bit elements; how exact they have to be, the bound alone decides.
A program may use at most 64 MiB of HBM per device.

v0:
```python
from functools import partial

import jax
import jax.numpy as jnp
from jax import lax
from jax.experimental import pallas as pl
from jax.experimental.pallas import tpu as pltpu
from jax.sharding import PartitionSpec as P

STEPS = 3
EIG_ITERS = 3
NS_ITERS = 8
F32 = jnp.float32
BF16 = jnp.bfloat16
NT = (((1,), (1,)), ((), ()))
MESH = pl.DeviceIdType.MESH


def dot(left, right):
    return jnp.dot(left, right, preferred_element_type=F32)


def left_mask(shape):
    return lax.broadcasted_iota(jnp.int32, shape, 1) < shape[1] // 2


def parts(wide):
    high = wide.astype(BF16)
    rest = wide - high.astype(F32)
    middle = rest.astype(BF16)
    last = rest - middle.astype(F32)
    return high, rest, middle, last


def as_left(twice):
    high, rest, middle, last = parts(twice)
    mask = left_mask(twice.shape)
    first = jnp.where(mask, twice, rest).astype(BF16)
    second = jnp.where(mask, twice, last).astype(BF16)
    return jnp.concatenate([first, first, second], axis=1)


def as_right(wide):
    high, rest, middle, last = parts(wide)
    return jnp.concatenate([high, high, middle, middle, last.astype(BF16), high], axis=0)


def as_right_transposed(twice):
    high, rest, middle, last = parts(twice)
    mask = left_mask(twice.shape)
    third = jnp.where(mask, last, twice).astype(BF16)
    rows = jnp.concatenate([high, middle, third], axis=1)
    return jnp.concatenate([rows, rows], axis=0)


def rotation_rows(gram):
    size = gram.shape[0]
    shape = gram.shape
    row = lax.broadcasted_iota(jnp.int32, shape, 0)
    column = lax.broadcasted_iota(jnp.int32, shape, 1)
    diagonal = (column == row) | (column == row + size)
    eye = jnp.where(diagonal, 1.0, 0.0).astype(F32)
    left = left_mask(shape)
    gram_right = as_right(gram)

    def polar_turn(step, carry):
        x, total = carry
        x_right = as_right(x)
        stacked = dot(jnp.concatenate([as_left(x), as_left(total)], axis=0), x_right)
        square = stacked[:size]
        total = total + 0.5 * stacked[size:]
        return 0.75 * square + 0.25 * dot(as_left(square), x_right), total

    def turn(index, z):
        z_left = as_left(z)
        inner = lax.dot_general(z_left, as_right_transposed(z), NT, preferred_element_type=F32)
        z_gram = dot(z_left, gram_right)
        squares = jnp.where(diagonal, inner, 0.0)
        scale_row = lax.rsqrt(jnp.sum(squares, axis=0, keepdims=True))
        scale_column = lax.rsqrt(0.5 * jnp.sum(squares, axis=1, keepdims=True))
        inner = inner * scale_column * scale_row
        bound = jnp.max(jnp.sum(jnp.abs(inner), axis=0, keepdims=True), axis=1, keepdims=True)
        x = eye - inner / bound
        both = jnp.where(left, z_gram, z) * (scale_column * lax.rsqrt(bound))
        x, total = lax.fori_loop(0, NS_ITERS - 1, polar_turn, (x, eye))
        both = dot(as_left(total), as_right(both))
        both = both + 0.5 * dot(as_left(x), as_right(both))
        other = pltpu.roll(both, size, 1)
        last = index == EIG_ITERS - 1
        return jnp.where(left == jnp.logical_not(last), both, other)

    return lax.fori_loop(0, EIG_ITERS, turn, gram)


def two_parts(values):
    high = values.astype(BF16)
    return high, (values - high.astype(F32)).astype(BF16)


def left_of_three(twice):
    rest = twice - twice.astype(BF16).astype(F32)
    first = jnp.where(left_mask(twice.shape), twice, rest).astype(BF16)
    return jnp.concatenate([first, twice.astype(BF16)], axis=1)[:, : 3 * twice.shape[1] // 2]


def right_of_three(values):
    high, low = two_parts(values)
    return jnp.concatenate([high, high, low], axis=0)


RAW = 2048
NEAR = 8
TILE = 512
STATE = 8
VMEM = pl.BlockSpec(memory_space=pltpu.VMEM)
SMEM = pl.BlockSpec(memory_space=pltpu.SMEM)
ANY = pl.BlockSpec(memory_space=pl.ANY)
DMA = pltpu.SemaphoreType.DMA


def at_tile(index, start=0):
    return pl.ds(pl.multiple_of(start + index * TILE, 128), TILE)


def gram_terms(first, second):
    pieces = jnp.concatenate(two_parts(jnp.concatenate([first, second], axis=0)), axis=0)
    return lax.dot_general(pieces, pieces, NT, preferred_element_type=F32)


def step_kernel(
    distance, first_ref, second_ref, terms_ref, state_ref,
    stay_ref, come_ref, next_terms_ref, next_state_ref,
    grams, raw_first, raw_second, rows_out, rows_in, move_out, near_sums, far_sums,
    near_send, near_recv, far_send, far_recv, gram_send, gram_recv, raw_send, raw_recv, rows_send, rows_recv, move_send, move_recv,
):
    me = lax.axis_index("rows")
    count = lax.axis_size("rows")
    here = lax.axis_index("blk")
    cycle = lax.axis_size("blk")
    target = lax.rem(here + distance, cycle)
    origin = lax.rem(here + (cycle - distance), cycle)
    width, columns = first_ref.shape
    size = 2 * width
    wide = 2 * size
    tiles = (columns - RAW) // TILE

    near, far = lax.rem(here, NEAR), here // NEAR
    groups = cycle // NEAR

    def row_peer(away):
        return {"rows": lax.rem(me + away, count)}

    def near_peer(away):
        return {"blk": far * NEAR + lax.rem(near + away, NEAR)}

    def far_peer(away):
        return {"blk": lax.rem(here + away * NEAR, cycle)}

    def each(peers, body):
        def one(away, carry):
            body(away)
            return carry

        lax.fori_loop(1, peers, one, 0)

    barrier = pltpu.get_barrier_semaphore()

    def greet(device):
        pl.semaphore_signal(barrier, inc=1, device_id=device, device_id_type=MESH)

    greet({"blk": origin})
    each(count, lambda away: greet(row_peer(away)))
    each(NEAR, lambda away: greet(near_peer(away)))
    each(groups, lambda away: greet(far_peer(away)))

    def shared(buffer, slot, device, send_sem, recv_sem, away):
        return pltpu.make_async_remote_copy(
            src_ref=buffer.at[slot], dst_ref=buffer.at[slot],
            send_sem=send_sem.at[away - 1], recv_sem=recv_sem.at[away - 1],
            device_id=device, device_id_type=MESH,
        )

    def gram_copy(away):
        return shared(grams, me, row_peer(away), gram_send, gram_recv, away)

    def near_copy(away):
        return shared(near_sums, near, near_peer(away), near_send, near_recv, away)

    def far_copy(away):
        return shared(far_sums, far, far_peer(away), far_send, far_recv, away)

    def to_target(source, destination, send_sem, recv_sem):
        return pltpu.make_async_remote_copy(
            src_ref=source, dst_ref=destination, send_sem=send_sem, recv_sem=recv_sem,
            device_id={"blk": target}, device_id_type=MESH,
        )

    end = pl.ds(columns - TILE, TILE)
    terms = terms_ref[...] + gram_terms(first_ref[:, end], second_ref[:, end])
    terms = terms[:size] + terms[size:]
    part = terms + pltpu.roll(terms, size, 1)
    left = left_mask((width, wide))
    grams[me] = jnp.where(left, part[:width], part[width:])

    pl.semaphore_wait(barrier, 1 + (count - 1) + (NEAR - 1) + (groups - 1))
    each(count, lambda away: gram_copy(away).start())
    raw = [
        to_target(first_ref.at[:, pl.ds(0, RAW)], raw_first, raw_send.at[0], raw_recv.at[0]),
        to_target(second_ref.at[:, pl.ds(0, RAW)], raw_second, raw_send.at[1], raw_recv.at[1]),
    ]
    for copy in raw:
        copy.start()
    each(count, lambda away: gram_copy(away).wait())
    packed = (grams[0] + grams[1]) + (grams[2] + grams[3])
    turned = pltpu.roll(packed, size, 1)
    gram = jnp.concatenate(
        [jnp.where(left, packed, turned), jnp.where(left, turned, packed)], axis=0
    )

    row = lax.broadcasted_iota(jnp.int32, gram.shape, 0)
    column = lax.broadcasted_iota(jnp.int32, gram.shape, 1)
    squares = jnp.where(column < size, gram * gram, 0.0)
    off = jnp.sum(jnp.where(column == row, 0.0, squares), axis=0, keepdims=True)
    diag = jnp.sum(jnp.where(column == row, squares, 0.0), axis=0, keepdims=True)
    near_sums[near] = jnp.concatenate([off, diag, jnp.zeros((6, wide), F32)], axis=0)
    each(NEAR, lambda away: near_copy(away).start())
    state = state_ref[...]
    flag = state[:1]

    rotation = rotation_rows(gram)
    top, bottom = rotation[:width], rotation[width:]
    staying = flag * bottom + (1.0 - flag) * top
    leaving = flag * top + (1.0 - flag) * bottom
    rows_out[...] = leaving
    rows_copy = to_target(rows_out, rows_in, rows_send, rows_recv)
    rows_copy.start()
    weights = left_of_three(jnp.concatenate([staying, leaving], axis=0))

    def move_copy(index):
        return to_target(
            move_out.at[:, at_tile(index)], come_ref.at[:, at_tile(index, RAW)],
            move_send.at[index], move_recv.at[index],
        )

    def rotate_tile(index, carry):
        tile = at_tile(index, RAW)
        current = jnp.concatenate([first_ref[:, tile], second_ref[:, tile]], axis=0)
        rotated = dot(weights, right_of_three(current))
        stay_ref[:, tile] = rotated[:width]
        move_out[:, at_tile(index)] = rotated[width:]

        @pl.when(index == tiles - 1)
        def _():
            each(NEAR, lambda away: near_copy(away).wait())
            far_sums[far] = jnp.sum(near_sums[...], axis=0)
            each(groups, lambda away: far_copy(away).start())

        move_copy(index).start()
        return carry

    lax.fori_loop(0, tiles, rotate_tile, 0)

    for copy in raw:
        copy.wait()
    rows_copy.wait()
    arrived = left_of_three(rows_in[...])

    def come_tile(index, total):
        tile = at_tile(index)
        current = jnp.concatenate([first_ref[:, tile], second_ref[:, tile]], axis=0)
        other = jnp.concatenate([raw_first[:, tile], raw_second[:, tile]], axis=0)
        stay = dot(weights[:width], right_of_three(current))
        come = dot(arrived, right_of_three(other))
        stay_ref[:, tile] = stay
        come_ref[:, tile] = come
        return total + gram_terms(stay, come)

    total = lax.fori_loop(0, RAW // TILE, come_tile, jnp.zeros((wide, wide), F32))

    def wait_tile(index, total):
        move_copy(index).wait()
        tile = at_tile(index, RAW)
        return total + gram_terms(stay_ref[:, tile], come_ref[:, tile])

    next_terms_ref[...] = lax.fori_loop(0, tiles - 1, wait_tile, total)
    each(groups, lambda away: far_copy(away).wait())
    roots = jnp.sqrt(jnp.sum(jnp.sum(far_sums[...], axis=0)[:2], axis=1, keepdims=True))
    ratio = jnp.broadcast_to(roots[:1] / roots[1:], flag.shape)
    next_state_ref[...] = jnp.concatenate([state[1 : STEPS + 1], flag, state[STEPS + 2 :], ratio], axis=0)
    move_copy(tiles - 1).wait()


def step(first, second, terms, state, distance):
    width, columns = first.shape
    block = jax.ShapeDtypeStruct((width, columns), F32)
    size = 2 * width
    tiles = (columns - RAW) // TILE
    return pl.pallas_call(
        partial(step_kernel, distance),
        out_shape=(
            block,
            block,
            jax.ShapeDtypeStruct((2 * size, 2 * size), F32),
            jax.ShapeDtypeStruct((STATE, 2 * size), F32),
        ),
        in_specs=[VMEM] * 4,
        out_specs=(VMEM,) * 4,
        scratch_shapes=[
            pltpu.VMEM((4, width, 2 * size), F32),
            pltpu.VMEM((width, RAW), F32),
            pltpu.VMEM((width, RAW), F32),
            pltpu.VMEM((width, 2 * size), F32),
            pltpu.VMEM((width, 2 * size), F32),
            pltpu.VMEM((width, columns - RAW), F32),
            pltpu.VMEM((NEAR, 8, 2 * size), F32),
            pltpu.VMEM((4, 8, 2 * size), F32),
            DMA((NEAR - 1,)), DMA((NEAR - 1,)), DMA((3,)), DMA((3,)),
            DMA((3,)), DMA((3,)), DMA((2,)), DMA((2,)), DMA, DMA, DMA((tiles,)), DMA((tiles,)),
        ],
        compiler_params=pltpu.CompilerParams(
            collective_id=distance, has_side_effects=True, vmem_limit_bytes=40 * 1024 * 1024
        ),
        name=f"step_{distance}",
    )(first, second, terms, state)


def begin_kernel(columns_ref, plan_any, first_ref, second_ref, terms_ref, state_ref, branch_any, plan_ref, branch_ref, sems):
    width, columns = first_ref.shape
    pieces = 4
    span = columns // pieces
    plan_copy = pltpu.make_async_copy(plan_any, plan_ref, sems.at[2 * pieces])
    plan_copy.start()
    copies = []
    for index in range(pieces):
        part = pl.ds(index * span, span)
        for half, block_ref in enumerate((first_ref, second_ref)):
            copy = pltpu.make_async_copy(
                columns_ref.at[pl.ds(half * width, width), part],
                block_ref.at[:, part],
                sems.at[2 * index + half],
            )
            copy.start()
            copies.append(copy)
    plan_copy.wait()
    rows = []
    slot = jnp.int32(0)
    for index in range(STEPS):
        stays = (plan_ref[index, 1] == 1).astype(jnp.int32)
        branch_ref[index] = jnp.maximum(plan_ref[index, 0] >> 1, plan_ref[index, 1] >> 1) - 1
        rows.append(jnp.full((1, 4 * width), ((1 - stays) == slot).astype(F32), F32))
        slot = stays
    rows.append(jnp.full((1, 4 * width), slot.astype(F32), F32))
    branch_copy = pltpu.make_async_copy(branch_ref, branch_any, sems.at[2 * pieces + 1])
    branch_copy.start()
    state_ref[...] = jnp.concatenate(rows + [jnp.zeros((STATE - STEPS - 1, 4 * width), F32)], axis=0)
    total = jnp.zeros((4 * width, 4 * width), F32)
    for index in range(pieces):
        copies[2 * index].wait()
        copies[2 * index + 1].wait()
        size = span if index < pieces - 1 else span - TILE
        part = pl.ds(index * span, size)
        total = total + gram_terms(first_ref[:, part], second_ref[:, part])
    terms_ref[...] = total
    branch_copy.wait()


def begin(columns, plan):
    width = columns.shape[0] // 2
    block = jax.ShapeDtypeStruct((width, columns.shape[1]), F32)
    return pl.pallas_call(
        begin_kernel,
        out_shape=(
            block,
            block,
            jax.ShapeDtypeStruct((4 * width, 4 * width), F32),
            jax.ShapeDtypeStruct((STATE, 4 * width), F32),
            jax.ShapeDtypeStruct((STEPS,), jnp.int32),
        ),
        in_specs=[ANY, ANY],
        out_specs=(VMEM,) * 4 + (ANY,),
        scratch_shapes=[
            pltpu.SMEM(plan.shape, jnp.int32), pltpu.SMEM((STEPS,), jnp.int32), DMA((10,)),
        ],
        name="begin",
    )(columns, plan)


def finish_kernel(first_ref, second_ref, state_ref, swept_ref, ratio_ref, ratios, sems):
    width = first_ref.shape[0]
    start = pl.multiple_of(state_ref[0, 0].astype(jnp.int32) * width, width)
    copies = [
        pltpu.make_async_copy(first_ref, swept_ref.at[pl.ds(start, width)], sems.at[0]),
        pltpu.make_async_copy(second_ref, swept_ref.at[pl.ds(width - start, width)], sems.at[1]),
    ]
    for copy in copies:
        copy.start()
    for index in range(STEPS):
        ratios[index] = state_ref[STATE - STEPS + index, 0]
    copies.append(pltpu.make_async_copy(ratios, ratio_ref, sems.at[2]))
    copies[-1].start()
    for copy in copies:
        copy.wait()


def finish(first, second, state):
    width, columns = first.shape
    return pl.pallas_call(
        finish_kernel,
        out_shape=(
            jax.ShapeDtypeStruct((2 * width, columns), F32),
            jax.ShapeDtypeStruct((STEPS,), F32),
        ),
        in_specs=[VMEM, VMEM, VMEM],
        out_specs=(ANY, ANY),
        scratch_shapes=[pltpu.SMEM((STEPS,), F32), DMA((3,))],
        name="finish",
    )(first, second, state)


def local(columns, plan):
    cycle = lax.axis_size("blk")
    branches = [partial(step, distance=distance) for distance in range(1, cycle)]
    *held, chosen = begin(columns, plan)

    def one_step(index, held):
        return tuple(lax.switch(chosen[index], branches, *held))

    first, second, terms, state = lax.fori_loop(0, STEPS, one_step, tuple(held))
    return tuple(finish(first, second, state))


def solution(mesh):
    return jax.shard_map(
        local,
        mesh=mesh,
        in_specs=(P("blk", "rows"), P()),
        out_specs=(P("blk", "rows"), P()),
        check_vma=False,
    )
```

profile of v0, /device:TPU:1, one launch (start us, length us, event | category | flops | bytes accessed | tf_op | source)
XLA Modules:
  0.0 82.1 jit_solution(3056925730447617977)
XLA Ops:
  0.6 2.0 %begin.1 = (f32[32,4096]{1,0:T(8,128)S(1)}, f32[32,4096]{1,0:T(8,128)S(1)}, f32[128,128]{1,0:T(8,128)S(1)}, f32[8,128]{1,0:T(8,128)S(1)}, s32[3]{0:T(128)S(1)}) custom-call(f32[64,4096]{1,0:T(8,128)} %columns_ref.1, s32[3,64]{1,0:T(4,128)} %plan_any.1), custom_call_target="tpu_custom_call" | custom-call | tf_op jit(solution)/shard_map/begin/pallas_call | solution.py:370
  2.6 78.4 %while.19 = (s32[]{:T(128)}, f32[32,4096]{1,0:T(8,128)S(1)}, f32[32,4096]{1,0:T(8,128)S(1)}, f32[128,128]{1,0:T(8,128)S(1)}, f32[8,128]{1,0:T(8,128)S(1)}, /*ind...) while((s32[]{:T(128)}, f32[32,4096]{1,0:T(8,128)S(1)}, f32[32,4096]{1,0:T(8,128)S(1)}, ...), condition=%wide.region_32.0_spmd, body=%wide.region_0.0_spmd.sunk | while | flops 3 | bytes 2236585 | solution.py:428
  2.6 0.6 dynamic_slice.8
  3.9 25.5 %conditional.2 = ((f32[32,4096]{1,0:T(8,128)S(1)}, f32[32,4096]{1,0:T(8,128)S(1)}, f32[128,128]{1,0:T(8,128)S(1)}, f32[8,128]{1,0:T(8,128)S(1)})) conditional(s32[]{:T(128)} %bitcast.2, (f32[32,4096]{1,0:T(8,128)S(1)}, f32[32,4096]{1,0:T(8,128)S(1)}, f32[128,128]{1,0:T(8,128)S(1)}, ...), branch_computations={%region_1.0_spmd, %region_2.0_spmd, %region_3.0_spmd, %region_4.0_... | conditional | bytes 8 | solution.py:426
  3.9 25.4 %step_23.1 = (f32[32,4096]{1,0:T(8,128)S(1)}, f32[32,4096]{1,0:T(8,128)S(1)}, f32[128,128]{1,0:T(8,128)S(1)}, f32[8,128]{1,0:T(8,128)S(1)}) custom-call(f32[32,4096]{1,0:T(8,128)S(1)} %get-tuple-element.445.first_ref, f32[32,4096]{1,0:T(8,128)S(1)} %get-tuple-element.446.second_ref, f32[128,128]{1,0:T(8,128)S(1)} %get-tuple-element.447.terms_ref, ...), custom_call_target="tpu_custom_call" | custom-call | tf_op jit(solution)/shard_map/while/body/eval_jaxpr/cond/branch_22_fun/step_23/pallas_call | solution.py:298
  29.5 0.6 dynamic_slice.8
  30.8 24.6 %conditional.2 = ((f32[32,4096]{1,0:T(8,128)S(1)}, f32[32,4096]{1,0:T(8,128)S(1)}, f32[128,128]{1,0:T(8,128)S(1)}, f32[8,128]{1,0:T(8,128)S(1)})) conditional(s32[]{:T(128)} %bitcast.2, (f32[32,4096]{1,0:T(8,128)S(1)}, f32[32,4096]{1,0:T(8,128)S(1)}, f32[128,128]{1,0:T(8,128)S(1)}, ...), branch_computations={%region_1.0_spmd, %region_2.0_spmd, %region_3.0_spmd, %region_4.0_... | conditional | bytes 8 | solution.py:426
  30.8 24.6 %step_7.1 = (f32[32,4096]{1,0:T(8,128)S(1)}, f32[32,4096]{1,0:T(8,128)S(1)}, f32[128,128]{1,0:T(8,128)S(1)}, f32[8,128]{1,0:T(8,128)S(1)}) custom-call(f32[32,4096]{1,0:T(8,128)S(1)} %get-tuple-element.381.first_ref, f32[32,4096]{1,0:T(8,128)S(1)} %get-tuple-element.382.second_ref, f32[128,128]{1,0:T(8,128)S(1)} %get-tuple-element.383.terms_ref, ...), custom_call_target="tpu_custom_call" | custom-call | tf_op jit(solution)/shard_map/while/body/eval_jaxpr/cond/branch_6_fun/step_7/pallas_call | solution.py:298
  55.5 0.6 dynamic_slice.8
  56.8 24.2 %conditional.2 = ((f32[32,4096]{1,0:T(8,128)S(1)}, f32[32,4096]{1,0:T(8,128)S(1)}, f32[128,128]{1,0:T(8,128)S(1)}, f32[8,128]{1,0:T(8,128)S(1)})) conditional(s32[]{:T(128)} %bitcast.2, (f32[32,4096]{1,0:T(8,128)S(1)}, f32[32,4096]{1,0:T(8,128)S(1)}, f32[128,128]{1,0:T(8,128)S(1)}, ...), branch_computations={%region_1.0_spmd, %region_2.0_spmd, %region_3.0_spmd, %region_4.0_... | conditional | bytes 8 | solution.py:426
  56.8 24.1 %step_27.1 = (f32[32,4096]{1,0:T(8,128)S(1)}, f32[32,4096]{1,0:T(8,128)S(1)}, f32[128,128]{1,0:T(8,128)S(1)}, f32[8,128]{1,0:T(8,128)S(1)}) custom-call(f32[32,4096]{1,0:T(8,128)S(1)} %get-tuple-element.461.first_ref, f32[32,4096]{1,0:T(8,128)S(1)} %get-tuple-element.462.second_ref, f32[128,128]{1,0:T(8,128)S(1)} %get-tuple-element.463.terms_ref, ...), custom_call_target="tpu_custom_call" | custom-call | tf_op jit(solution)/shard_map/while/body/eval_jaxpr/cond/branch_26_fun/step_27/pallas_call | solution.py:298
  81.0 1.0 %finish.1 = (f32[64,4096]{1,0:T(8,128)}, f32[3]{0:T(128)}) custom-call(f32[32,4096]{1,0:T(8,128)S(1)} %get-tuple-element.507.first_ref, f32[32,4096]{1,0:T(8,128)S(1)} %get-tuple-element.508.second_ref, f32[8,128]{1,0:T(8,128)S(1)} %get-tuple-element.509.state_ref), custom_call_target="tpu_custom_call" | custom-call | tf_op jit(solution)/shard_map/finish/pallas_call | solution.py:407
  (12 shorter events, 0.2 us)
where the time goes:
time: 83.1 us; the launch traced here: 82.1 us
  Pallas kernels  77.1 us (93%)
  loops' own time  2.34 us (3%)
  local copies, waits for them, and re-layouts  2 us (2%)
    pallas_call x3, Pallas kernels, step(): pl.pallas_call(partial(step_kernel, distance), out_shape=(block, block, j...  74.1 us
    another operation x1, loops' own time, local(): first, second, terms, state = lax.fori_loop(0, STEPS, one_step, tuple(held))  2.12 us
    pallas_call x1, Pallas kernels, begin(): pl.pallas_call(begin_kernel, out_shape=(block, block, jax.ShapeDtypeStruc...  1.99 us
    dynamic_slice x3, local copies, waits for them, and re-layouts, one_step(): return tuple(lax.switch(chosen[index], branches, *held))  1.76 us

commit v1 on v0

--- a/solution.py
+++ b/solution.py
@@ -53,7 +53,7 @@
     return jnp.concatenate([rows, rows], axis=0)
 
 
-def rotation_rows(gram):
+def rotation_rows(gram, between):
     size = gram.shape[0]
     shape = gram.shape
     row = lax.broadcasted_iota(jnp.int32, shape, 0)
@@ -72,6 +72,7 @@
         return 0.75 * square + 0.25 * dot(as_left(square), x_right), total
 
     def turn(index, z):
+        between(index)
         z_left = as_left(z)
         inner = lax.dot_general(z_left, as_right_transposed(z), NT, preferred_element_type=F32)
         z_gram = dot(z_left, gram_right)
@@ -110,8 +111,9 @@
 
 RAW = 2048
 NEAR = 8
+CORES = 2
 TILE = 512
-STATE = 8
+STATE = 16
 VMEM = pl.BlockSpec(memory_space=pltpu.VMEM)
 SMEM = pl.BlockSpec(memory_space=pltpu.SMEM)
 ANY = pl.BlockSpec(memory_space=pl.ANY)
@@ -130,7 +132,8 @@
 def step_kernel(
     distance, first_ref, second_ref, terms_ref, state_ref,
     stay_ref, come_ref, next_terms_ref, next_state_ref,
-    grams, raw_first, raw_second, rows_out, rows_in, move_out, near_sums, far_sums,
+    grams, raw_first, raw_second, rows_out, rows_in, move_out, core_sums, near_sums, far_sums,
+    core_send, core_recv,
     near_send, near_recv, far_send, far_recv, gram_send, gram_recv, raw_send, raw_recv, rows_send, rows_recv, move_send, move_recv,
 ):
     me = lax.axis_index("rows")
@@ -144,14 +147,17 @@
     wide = 2 * size
     tiles = (columns - RAW) // TILE
 
-    near, far = lax.rem(here, NEAR), here // NEAR
-    groups = cycle // NEAR
+    core, near, far = lax.rem(here, CORES), lax.rem(here, NEAR) // CORES, here // NEAR
+    line, groups = NEAR // CORES, cycle // NEAR
 
     def row_peer(away):
         return {"rows": lax.rem(me + away, count)}
 
     def near_peer(away):
-        return {"blk": far * NEAR + lax.rem(near + away, NEAR)}
+        return {"blk": far * NEAR + lax.rem(near + away, line) * CORES + core}
+
+    def core_peer(away):
+        return {"blk": here + away - 2 * core}
 
     def far_peer(away):
         return {"blk": lax.rem(here + away * NEAR, cycle)}
@@ -170,7 +176,8 @@
 
     greet({"blk": origin})
     each(count, lambda away: greet(row_peer(away)))
-    each(NEAR, lambda away: greet(near_peer(away)))
+    greet(core_peer(1))
+    each(line, lambda away: greet(near_peer(away)))
     each(groups, lambda away: greet(far_peer(away)))
 
     def shared(buffer, slot, device, send_sem, recv_sem, away):
@@ -183,6 +190,9 @@
     def gram_copy(away):
         return shared(grams, me, row_peer(away), gram_send, gram_recv, away)
 
+    def core_copy(away):
+        return shared(core_sums, core, core_peer(away), core_send, core_recv, away)
+
     def near_copy(away):
         return shared(near_sums, near, near_peer(away), near_send, near_recv, away)
 
@@ -202,7 +212,7 @@
     left = left_mask((width, wide))
     grams[me] = jnp.where(left, part[:width], part[width:])
 
-    pl.semaphore_wait(barrier, 1 + (count - 1) + (NEAR - 1) + (groups - 1))
+    pl.semaphore_wait(barrier, 1 + (count - 1) + (CORES - 1) + (line - 1) + (groups - 1))
     each(count, lambda away: gram_copy(away).start())
     raw = [
         to_target(first_ref.at[:, pl.ds(0, RAW)], raw_first, raw_send.at[0], raw_recv.at[0]),
@@ -222,12 +232,19 @@
     squares = jnp.where(column < size, gram * gram, 0.0)
     off = jnp.sum(jnp.where(column == row, 0.0, squares), axis=0, keepdims=True)
     diag = jnp.sum(jnp.where(column == row, squares, 0.0), axis=0, keepdims=True)
-    near_sums[near] = jnp.concatenate([off, diag, jnp.zeros((6, wide), F32)], axis=0)
-    each(NEAR, lambda away: near_copy(away).start())
+    core_sums[core] = jnp.concatenate([off, diag, jnp.zeros((6, wide), F32)], axis=0)
+    core_copy(1).start()
     state = state_ref[...]
     flag = state[:1]
 
-    rotation = rotation_rows(gram)
+    def between(index):
+        @pl.when(index == 1)
+        def _():
+            core_copy(1).wait()
+            near_sums[near] = core_sums[0] + core_sums[1]
+            each(line, lambda away: near_copy(away).start())
+
+    rotation = rotation_rows(gram, between)
     top, bottom = rotation[:width], rotation[width:]
     staying = flag * bottom + (1.0 - flag) * top
     leaving = flag * top + (1.0 - flag) * bottom
@@ -251,7 +268,7 @@
 
         @pl.when(index == tiles - 1)
         def _():
-            each(NEAR, lambda away: near_copy(away).wait())
+            each(line, lambda away: near_copy(away).wait())
             far_sums[far] = jnp.sum(near_sums[...], axis=0)
             each(groups, lambda away: far_copy(away).start())
 
@@ -284,9 +301,10 @@
 
     next_terms_ref[...] = lax.fori_loop(0, tiles - 1, wait_tile, total)
     each(groups, lambda away: far_copy(away).wait())
-    roots = jnp.sqrt(jnp.sum(jnp.sum(far_sums[...], axis=0)[:2], axis=1, keepdims=True))
-    ratio = jnp.broadcast_to(roots[:1] / roots[1:], flag.shape)
-    next_state_ref[...] = jnp.concatenate([state[1 : STEPS + 1], flag, state[STEPS + 2 :], ratio], axis=0)
+    totals = jnp.sum(far_sums[...], axis=0)
+    next_state_ref[...] = jnp.concatenate(
+        [state[1 : STEPS + 1], flag, state[STEPS + 1 : 8], state[10:], totals[:2]], axis=0
+    )
     move_copy(tiles - 1).wait()
 
 
@@ -312,9 +330,10 @@
             pltpu.VMEM((width, 2 * size), F32),
             pltpu.VMEM((width, 2 * size), F32),
             pltpu.VMEM((width, columns - RAW), F32),
-            pltpu.VMEM((NEAR, 8, 2 * size), F32),
+            pltpu.VMEM((CORES, 8, 2 * size), F32),
+            pltpu.VMEM((NEAR // CORES, 8, 2 * size), F32),
             pltpu.VMEM((4, 8, 2 * size), F32),
-            DMA((NEAR - 1,)), DMA((NEAR - 1,)), DMA((3,)), DMA((3,)),
+            DMA((1,)), DMA((1,)), DMA((3,)), DMA((3,)), DMA((3,)), DMA((3,)),
             DMA((3,)), DMA((3,)), DMA((2,)), DMA((2,)), DMA, DMA, DMA((tiles,)), DMA((tiles,)),
         ],
         compiler_params=pltpu.CompilerParams(
@@ -394,8 +413,10 @@
     ]
     for copy in copies:
         copy.start()
+    roots = jnp.sqrt(jnp.sum(state_ref[STATE - 8 :], axis=1, keepdims=True))
     for index in range(STEPS):
-        ratios[index] = state_ref[STATE - STEPS + index, 0]
+        row = 8 - 2 * (STEPS - index)
+        ratios[index] = (roots[row : row + 1] / roots[row + 1 : row + 2])[0, 0]
     copies.append(pltpu.make_async_copy(ratios, ratio_ref, sems.at[2]))
     copies[-1].start()
     for copy in copies:

time: 83.1 us -> 82.3 us (level)
  the two profiles are of different devices: /device:TPU:1 before, /device:TPU:6 now
where the time goes in v1:
time: 82.3 us; the launch traced here: 82.4 us
  Pallas kernels  77.5 us (94%)
  loops' own time  2.34 us (3%)
  local copies, waits for them, and re-layouts  2 us (2%)
    pallas_call x3, Pallas kernels, step(): pl.pallas_call(partial(step_kernel, distance), out_shape=(block, block, j...  74.4 us
    another operation x1, loops' own time, local(): first, second, terms, state = lax.fori_loop(0, STEPS, one_step, tuple(held))  2.12 us
    pallas_call x1, Pallas kernels, begin(): pl.pallas_call(begin_kernel, out_shape=(block, block, jax.ShapeDtypeStruc...  1.99 us
    dynamic_slice x3, local copies, waits for them, and re-layouts, one_step(): return tuple(lax.switch(chosen[index], branches, *held))  1.76 us

profile of v1, /device:TPU:6, one launch (start us, length us, event | category | flops | bytes accessed | tf_op | source)
XLA Modules:
  0.0 82.4 jit_solution(14417495815473049009)
XLA Ops:
  0.6 2.0 %begin.1 = (f32[32,4096]{1,0:T(8,128)S(1)}, f32[32,4096]{1,0:T(8,128)S(1)}, f32[128,128]{1,0:T(8,128)S(1)}, f32[16,128]{1,0:T(8,128)S(1)}, s32[3]{0:T(128)S(1)}) custom-call(f32[64,4096]{1,0:T(8,128)} %columns_ref.1, s32[3,64]{1,0:T(4,128)} %plan_any.1), custom_call_target="tpu_custom_call" | custom-call | tf_op jit(solution)/shard_map/begin/pallas_call | solution.py:389
  2.6 78.8 %while.19 = (s32[]{:T(128)}, f32[32,4096]{1,0:T(8,128)S(1)}, f32[32,4096]{1,0:T(8,128)S(1)}, f32[128,128]{1,0:T(8,128)S(1)}, f32[16,128]{1,0:T(8,128)S(1)}, /*in...) while((s32[]{:T(128)}, f32[32,4096]{1,0:T(8,128)S(1)}, f32[32,4096]{1,0:T(8,128)S(1)}, ...), condition=%wide.region_32.0_spmd, body=%wide.region_0.0_spmd.sunk | while | flops 3 | bytes 2244777 | solution.py:449
  2.6 0.6 dynamic_slice.8
  3.9 25.4 %conditional.2 = ((f32[32,4096]{1,0:T(8,128)S(1)}, f32[32,4096]{1,0:T(8,128)S(1)}, f32[128,128]{1,0:T(8,128)S(1)}, f32[16,128]{1,0:T(8,128)S(1)})) conditional(s32[]{:T(128)} %bitcast.2, (f32[32,4096]{1,0:T(8,128)S(1)}, f32[32,4096]{1,0:T(8,128)S(1)}, f32[128,128]{1,0:T(8,128)S(1)}, ...), branch_computations={%region_1.0_spmd, %region_2.0_spmd, %region_3.0_spmd, %region_4.0_... | conditional | bytes 8 | solution.py:447
  3.9 25.3 %step_16.1 = (f32[32,4096]{1,0:T(8,128)S(1)}, f32[32,4096]{1,0:T(8,128)S(1)}, f32[128,128]{1,0:T(8,128)S(1)}, f32[16,128]{1,0:T(8,128)S(1)}) custom-call(f32[32,4096]{1,0:T(8,128)S(1)} %get-tuple-element.417.first_ref, f32[32,4096]{1,0:T(8,128)S(1)} %get-tuple-element.418.second_ref, f32[128,128]{1,0:T(8,128)S(1)} %get-tuple-element.419.terms_ref, ...), custom_call_target="tpu_custom_call" | custom-call | tf_op jit(solution)/shard_map/while/body/eval_jaxpr/cond/branch_15_fun/step_16/pallas_call | solution.py:316
  29.4 0.6 dynamic_slice.8
  30.6 24.6 %conditional.2 = ((f32[32,4096]{1,0:T(8,128)S(1)}, f32[32,4096]{1,0:T(8,128)S(1)}, f32[128,128]{1,0:T(8,128)S(1)}, f32[16,128]{1,0:T(8,128)S(1)})) conditional(s32[]{:T(128)} %bitcast.2, (f32[32,4096]{1,0:T(8,128)S(1)}, f32[32,4096]{1,0:T(8,128)S(1)}, f32[128,128]{1,0:T(8,128)S(1)}, ...), branch_computations={%region_1.0_spmd, %region_2.0_spmd, %region_3.0_spmd, %region_4.0_... | conditional | bytes 8 | solution.py:447
  30.7 24.6 %step_19.1 = (f32[32,4096]{1,0:T(8,128)S(1)}, f32[32,4096]{1,0:T(8,128)S(1)}, f32[128,128]{1,0:T(8,128)S(1)}, f32[16,128]{1,0:T(8,128)S(1)}) custom-call(f32[32,4096]{1,0:T(8,128)S(1)} %get-tuple-element.429.first_ref, f32[32,4096]{1,0:T(8,128)S(1)} %get-tuple-element.430.second_ref, f32[128,128]{1,0:T(8,128)S(1)} %get-tuple-element.431.terms_ref, ...), custom_call_target="tpu_custom_call" | custom-call | tf_op jit(solution)/shard_map/while/body/eval_jaxpr/cond/branch_18_fun/step_19/pallas_call | solution.py:316
  55.4 0.6 dynamic_slice.8
  56.6 24.7 %conditional.2 = ((f32[32,4096]{1,0:T(8,128)S(1)}, f32[32,4096]{1,0:T(8,128)S(1)}, f32[128,128]{1,0:T(8,128)S(1)}, f32[16,128]{1,0:T(8,128)S(1)})) conditional(s32[]{:T(128)} %bitcast.2, (f32[32,4096]{1,0:T(8,128)S(1)}, f32[32,4096]{1,0:T(8,128)S(1)}, f32[128,128]{1,0:T(8,128)S(1)}, ...), branch_computations={%region_1.0_spmd, %region_2.0_spmd, %region_3.0_spmd, %region_4.0_... | conditional | bytes 8 | solution.py:447
  56.7 24.6 %step_22.1 = (f32[32,4096]{1,0:T(8,128)S(1)}, f32[32,4096]{1,0:T(8,128)S(1)}, f32[128,128]{1,0:T(8,128)S(1)}, f32[16,128]{1,0:T(8,128)S(1)}) custom-call(f32[32,4096]{1,0:T(8,128)S(1)} %get-tuple-element.441.first_ref, f32[32,4096]{1,0:T(8,128)S(1)} %get-tuple-element.442.second_ref, f32[128,128]{1,0:T(8,128)S(1)} %get-tuple-element.443.terms_ref, ...), custom_call_target="tpu_custom_call" | custom-call | tf_op jit(solution)/shard_map/while/body/eval_jaxpr/cond/branch_21_fun/step_22/pallas_call | solution.py:316
  81.4 1.0 %finish.1 = (f32[64,4096]{1,0:T(8,128)}, f32[3]{0:T(128)}) custom-call(f32[32,4096]{1,0:T(8,128)S(1)} %get-tuple-element.507.first_ref, f32[32,4096]{1,0:T(8,128)S(1)} %get-tuple-element.508.second_ref, f32[16,128]{1,0:T(8,128)S(1)} %get-tuple-element.509.state_ref), custom_call_target="tpu_custom_call" | custom-call | tf_op jit(solution)/shard_map/finish/pallas_call | solution.py:428
  (12 shorter events, 0.2 us)

commit v2 on v1

--- a/solution.py
+++ b/solution.py
@@ -345,7 +345,7 @@
 
 def begin_kernel(columns_ref, plan_any, first_ref, second_ref, terms_ref, state_ref, branch_any, plan_ref, branch_ref, sems):
     width, columns = first_ref.shape
-    pieces = 4
+    pieces = 2
     span = columns // pieces
     plan_copy = pltpu.make_async_copy(plan_any, plan_ref, sems.at[2 * pieces])
     plan_copy.start()

time: 82.3 us -> 80.1 us (0.973)
  the two profiles are of different devices: /device:TPU:6 before, /device:TPU:1 now
where the time goes in v2:
time: 80.1 us; the launch traced here: 79.7 us
  Pallas kernels  74.7 us (93%)
  loops' own time  2.34 us (3%)
  local copies, waits for them, and re-layouts  2 us (2%)
    pallas_call x3, Pallas kernels, step(): pl.pallas_call(partial(step_kernel, distance), out_shape=(block, block, j...  71.9 us
    another operation x1, loops' own time, local(): first, second, terms, state = lax.fori_loop(0, STEPS, one_step, tuple(held))  2.12 us
    dynamic_slice x3, local copies, waits for them, and re-layouts, one_step(): return tuple(lax.switch(chosen[index], branches, *held))  1.76 us
    pallas_call x1, Pallas kernels, begin(): pl.pallas_call(begin_kernel, out_shape=(block, block, jax.ShapeDtypeStruc...  1.7 us

profile of v2, /device:TPU:1, one launch (start us, length us, event | category | flops | bytes accessed | tf_op | source)
XLA Modules:
  0.0 79.7 jit_solution(6506601411217021191)
XLA Ops:
  0.6 1.7 %begin.1 = (f32[32,4096]{1,0:T(8,128)S(1)}, f32[32,4096]{1,0:T(8,128)S(1)}, f32[128,128]{1,0:T(8,128)S(1)}, f32[16,128]{1,0:T(8,128)S(1)}, s32[3]{0:T(128)S(1)}) custom-call(f32[64,4096]{1,0:T(8,128)} %columns_ref.1, s32[3,64]{1,0:T(4,128)} %plan_any.1), custom_call_target="tpu_custom_call" | custom-call | tf_op jit(solution)/shard_map/begin/pallas_call | solution.py:389
  2.3 76.3 %while.19 = (s32[]{:T(128)}, f32[32,4096]{1,0:T(8,128)S(1)}, f32[32,4096]{1,0:T(8,128)S(1)}, f32[128,128]{1,0:T(8,128)S(1)}, f32[16,128]{1,0:T(8,128)S(1)}, /*in...) while((s32[]{:T(128)}, f32[32,4096]{1,0:T(8,128)S(1)}, f32[32,4096]{1,0:T(8,128)S(1)}, ...), condition=%wide.region_32.0_spmd, body=%wide.region_0.0_spmd.sunk | while | flops 3 | bytes 2244777 | solution.py:449
  2.4 0.6 dynamic_slice.8
  3.6 25.8 %conditional.2 = ((f32[32,4096]{1,0:T(8,128)S(1)}, f32[32,4096]{1,0:T(8,128)S(1)}, f32[128,128]{1,0:T(8,128)S(1)}, f32[16,128]{1,0:T(8,128)S(1)})) conditional(s32[]{:T(128)} %bitcast.2, (f32[32,4096]{1,0:T(8,128)S(1)}, f32[32,4096]{1,0:T(8,128)S(1)}, f32[128,128]{1,0:T(8,128)S(1)}, ...), branch_computations={%region_1.0_spmd, %region_2.0_spmd, %region_3.0_spmd, %region_4.0_... | conditional | bytes 8 | solution.py:447
  3.6 25.7 %step_6.1 = (f32[32,4096]{1,0:T(8,128)S(1)}, f32[32,4096]{1,0:T(8,128)S(1)}, f32[128,128]{1,0:T(8,128)S(1)}, f32[16,128]{1,0:T(8,128)S(1)}) custom-call(f32[32,4096]{1,0:T(8,128)S(1)} %get-tuple-element.377.first_ref, f32[32,4096]{1,0:T(8,128)S(1)} %get-tuple-element.378.second_ref, f32[128,128]{1,0:T(8,128)S(1)} %get-tuple-element.379.terms_ref, ...), custom_call_target="tpu_custom_call" | custom-call | tf_op jit(solution)/shard_map/while/body/eval_jaxpr/cond/branch_5_fun/step_6/pallas_call | solution.py:316
  29.5 0.6 dynamic_slice.8
  30.8 25.8 %conditional.2 = ((f32[32,4096]{1,0:T(8,128)S(1)}, f32[32,4096]{1,0:T(8,128)S(1)}, f32[128,128]{1,0:T(8,128)S(1)}, f32[16,128]{1,0:T(8,128)S(1)})) conditional(s32[]{:T(128)} %bitcast.2, (f32[32,4096]{1,0:T(8,128)S(1)}, f32[32,4096]{1,0:T(8,128)S(1)}, f32[128,128]{1,0:T(8,128)S(1)}, ...), branch_computations={%region_1.0_spmd, %region_2.0_spmd, %region_3.0_spmd, %region_4.0_... | conditional | bytes 8 | solution.py:447
  30.8 25.7 %step_9.1 = (f32[32,4096]{1,0:T(8,128)S(1)}, f32[32,4096]{1,0:T(8,128)S(1)}, f32[128,128]{1,0:T(8,128)S(1)}, f32[16,128]{1,0:T(8,128)S(1)}) custom-call(f32[32,4096]{1,0:T(8,128)S(1)} %get-tuple-element.389.first_ref, f32[32,4096]{1,0:T(8,128)S(1)} %get-tuple-element.390.second_ref, f32[128,128]{1,0:T(8,128)S(1)} %get-tuple-element.391.terms_ref, ...), custom_call_target="tpu_custom_call" | custom-call | tf_op jit(solution)/shard_map/while/body/eval_jaxpr/cond/branch_8_fun/step_9/pallas_call | solution.py:316
  56.7 0.6 dynamic_slice.8
  57.9 20.5 %conditional.2 = ((f32[32,4096]{1,0:T(8,128)S(1)}, f32[32,4096]{1,0:T(8,128)S(1)}, f32[128,128]{1,0:T(8,128)S(1)}, f32[16,128]{1,0:T(8,128)S(1)})) conditional(s32[]{:T(128)} %bitcast.2, (f32[32,4096]{1,0:T(8,128)S(1)}, f32[32,4096]{1,0:T(8,128)S(1)}, f32[128,128]{1,0:T(8,128)S(1)}, ...), branch_computations={%region_1.0_spmd, %region_2.0_spmd, %region_3.0_spmd, %region_4.0_... | conditional | bytes 8 | solution.py:447
  58.0 20.5 %step_29.1 = (f32[32,4096]{1,0:T(8,128)S(1)}, f32[32,4096]{1,0:T(8,128)S(1)}, f32[128,128]{1,0:T(8,128)S(1)}, f32[16,128]{1,0:T(8,128)S(1)}) custom-call(f32[32,4096]{1,0:T(8,128)S(1)} %get-tuple-element.469.first_ref, f32[32,4096]{1,0:T(8,128)S(1)} %get-tuple-element.470.second_ref, f32[128,128]{1,0:T(8,128)S(1)} %get-tuple-element.471.terms_ref, ...), custom_call_target="tpu_custom_call" | custom-call | tf_op jit(solution)/shard_map/while/body/eval_jaxpr/cond/branch_28_fun/step_29/pallas_call | solution.py:316
  78.6 1.0 %finish.1 = (f32[64,4096]{1,0:T(8,128)}, f32[3]{0:T(128)}) custom-call(f32[32,4096]{1,0:T(8,128)S(1)} %get-tuple-element.507.first_ref, f32[32,4096]{1,0:T(8,128)S(1)} %get-tuple-element.508.second_ref, f32[16,128]{1,0:T(8,128)S(1)} %get-tuple-element.509.state_ref), custom_call_target="tpu_custom_call" | custom-call | tf_op jit(solution)/shard_map/finish/pallas_call | solution.py:428
  (12 shorter events, 0.2 us)

commit v3 on v2

--- a/solution.py
+++ b/solution.py
@@ -174,11 +174,11 @@
     def greet(device):
         pl.semaphore_signal(barrier, inc=1, device_id=device, device_id_type=MESH)
 
+    each(groups, lambda away: greet(far_peer(away)))
+    each(count, lambda away: greet(row_peer(away)))
     greet({"blk": origin})
-    each(count, lambda away: greet(row_peer(away)))
     greet(core_peer(1))
     each(line, lambda away: greet(near_peer(away)))
-    each(groups, lambda away: greet(far_peer(away)))
 
     def shared(buffer, slot, device, send_sem, recv_sem, away):
         return pltpu.make_async_remote_copy(

time: 80.1 us -> 80.9 us (level)
  no operation moved by 1% of the time
where the time goes in v3:
time: 80.9 us; the launch traced here: 79.7 us
  Pallas kernels  74.7 us (92%)
  loops' own time  2.32 us (3%)
  local copies, waits for them, and re-layouts  2 us (2%)
    pallas_call x3, Pallas kernels, step(): pl.pallas_call(partial(step_kernel, distance), out_shape=(block, block, j...  72 us
    another operation x1, loops' own time, local(): first, second, terms, state = lax.fori_loop(0, STEPS, one_step, tuple(held))  2.12 us
    dynamic_slice x3, local copies, waits for them, and re-layouts, one_step(): return tuple(lax.switch(chosen[index], branches, *held))  1.76 us
    pallas_call x1, Pallas kernels, begin(): pl.pallas_call(begin_kernel, out_shape=(block, block, jax.ShapeDtypeStruc...  1.7 us

profile of v3, /device:TPU:1, one launch (start us, length us, event | category | flops | bytes accessed | tf_op | source)
XLA Modules:
  0.0 79.7 jit_solution(13725123431130287317)
XLA Ops:
  0.6 1.7 %begin.1 = (f32[32,4096]{1,0:T(8,128)S(1)}, f32[32,4096]{1,0:T(8,128)S(1)}, f32[128,128]{1,0:T(8,128)S(1)}, f32[16,128]{1,0:T(8,128)S(1)}, s32[3]{0:T(128)S(1)}) custom-call(f32[64,4096]{1,0:T(8,128)} %columns_ref.1, s32[3,64]{1,0:T(4,128)} %plan_any.1), custom_call_target="tpu_custom_call" | custom-call | tf_op jit(solution)/shard_map/begin/pallas_call | solution.py:389
  2.3 76.3 %while.19 = (s32[]{:T(128)}, f32[32,4096]{1,0:T(8,128)S(1)}, f32[32,4096]{1,0:T(8,128)S(1)}, f32[128,128]{1,0:T(8,128)S(1)}, f32[16,128]{1,0:T(8,128)S(1)}, /*in...) while((s32[]{:T(128)}, f32[32,4096]{1,0:T(8,128)S(1)}, f32[32,4096]{1,0:T(8,128)S(1)}, ...), condition=%wide.region_32.0_spmd, body=%wide.region_0.0_spmd.sunk | while | flops 3 | bytes 2244777 | solution.py:449
  2.4 0.6 dynamic_slice.8
  3.6 23.2 %conditional.2 = ((f32[32,4096]{1,0:T(8,128)S(1)}, f32[32,4096]{1,0:T(8,128)S(1)}, f32[128,128]{1,0:T(8,128)S(1)}, f32[16,128]{1,0:T(8,128)S(1)})) conditional(s32[]{:T(128)} %bitcast.2, (f32[32,4096]{1,0:T(8,128)S(1)}, f32[32,4096]{1,0:T(8,128)S(1)}, f32[128,128]{1,0:T(8,128)S(1)}, ...), branch_computations={%region_1.0_spmd, %region_2.0_spmd, %region_3.0_spmd, %region_4.0_... | conditional | bytes 8 | solution.py:447
  3.6 23.2 %step_1.1 = (f32[32,4096]{1,0:T(8,128)S(1)}, f32[32,4096]{1,0:T(8,128)S(1)}, f32[128,128]{1,0:T(8,128)S(1)}, f32[16,128]{1,0:T(8,128)S(1)}) custom-call(f32[32,4096]{1,0:T(8,128)S(1)} %get-tuple-element.357.first_ref, f32[32,4096]{1,0:T(8,128)S(1)} %get-tuple-element.358.second_ref, f32[128,128]{1,0:T(8,128)S(1)} %get-tuple-element.359.terms_ref, ...), custom_call_target="tpu_custom_call" | custom-call | tf_op jit(solution)/shard_map/while/body/eval_jaxpr/cond/branch_0_fun/step_1/pallas_call | solution.py:316
  27.0 0.6 dynamic_slice.8
  28.2 23.6 %conditional.2 = ((f32[32,4096]{1,0:T(8,128)S(1)}, f32[32,4096]{1,0:T(8,128)S(1)}, f32[128,128]{1,0:T(8,128)S(1)}, f32[16,128]{1,0:T(8,128)S(1)})) conditional(s32[]{:T(128)} %bitcast.2, (f32[32,4096]{1,0:T(8,128)S(1)}, f32[32,4096]{1,0:T(8,128)S(1)}, f32[128,128]{1,0:T(8,128)S(1)}, ...), branch_computations={%region_1.0_spmd, %region_2.0_spmd, %region_3.0_spmd, %region_4.0_... | conditional | bytes 8 | solution.py:447
  28.2 23.6 %step_4.1 = (f32[32,4096]{1,0:T(8,128)S(1)}, f32[32,4096]{1,0:T(8,128)S(1)}, f32[128,128]{1,0:T(8,128)S(1)}, f32[16,128]{1,0:T(8,128)S(1)}) custom-call(f32[32,4096]{1,0:T(8,128)S(1)} %get-tuple-element.369.first_ref, f32[32,4096]{1,0:T(8,128)S(1)} %get-tuple-element.370.second_ref, f32[128,128]{1,0:T(8,128)S(1)} %get-tuple-element.371.terms_ref, ...), custom_call_target="tpu_custom_call" | custom-call | tf_op jit(solution)/shard_map/while/body/eval_jaxpr/cond/branch_3_fun/step_4/pallas_call | solution.py:316
  52.0 0.6 dynamic_slice.8
  53.2 25.3 %conditional.2 = ((f32[32,4096]{1,0:T(8,128)S(1)}, f32[32,4096]{1,0:T(8,128)S(1)}, f32[128,128]{1,0:T(8,128)S(1)}, f32[16,128]{1,0:T(8,128)S(1)})) conditional(s32[]{:T(128)} %bitcast.2, (f32[32,4096]{1,0:T(8,128)S(1)}, f32[32,4096]{1,0:T(8,128)S(1)}, f32[128,128]{1,0:T(8,128)S(1)}, ...), branch_computations={%region_1.0_spmd, %region_2.0_spmd, %region_3.0_spmd, %region_4.0_... | conditional | bytes 8 | solution.py:447
  53.3 25.2 %step_27.1 = (f32[32,4096]{1,0:T(8,128)S(1)}, f32[32,4096]{1,0:T(8,128)S(1)}, f32[128,128]{1,0:T(8,128)S(1)}, f32[16,128]{1,0:T(8,128)S(1)}) custom-call(f32[32,4096]{1,0:T(8,128)S(1)} %get-tuple-element.461.first_ref, f32[32,4096]{1,0:T(8,128)S(1)} %get-tuple-element.462.second_ref, f32[128,128]{1,0:T(8,128)S(1)} %get-tuple-element.463.terms_ref, ...), custom_call_target="tpu_custom_call" | custom-call | tf_op jit(solution)/shard_map/while/body/eval_jaxpr/cond/branch_26_fun/step_27/pallas_call | solution.py:316
  78.6 1.0 %finish.1 = (f32[64,4096]{1,0:T(8,128)}, f32[3]{0:T(128)}) custom-call(f32[32,4096]{1,0:T(8,128)S(1)} %get-tuple-element.507.first_ref, f32[32,4096]{1,0:T(8,128)S(1)} %get-tuple-element.508.second_ref, f32[16,128]{1,0:T(8,128)S(1)} %get-tuple-element.509.state_ref), custom_call_target="tpu_custom_call" | custom-call | tf_op jit(solution)/shard_map/finish/pallas_call | solution.py:428
  (12 shorter events, 0.2 us)
